TPU v7x, 32 devices: a whole 2x2x4 slice. The times are simulated.
32 devices in a mesh: row: 4 (over y, x), col: 8 (over z, core).
Axes of the slice: x: 2, y: 2, z: 4, core: 2. Of those that a mesh axis runs over, the one named last changes fastest.
Arguments:
- start_vector: bfloat16 [4, 2048, 2048], P(None, 'row', 'col'), may hold values from -150 to 150
- left_env: bfloat16 [5, 2048, 2048], P(None, 'row', 'col'), may hold values from -5 to 6
- right_env: bfloat16 [5, 2048, 2048], P(None, 'col', 'row'), may hold values from -5 to 6
- left_tensor: float32 [5, 5, 2, 2], replicated, may hold values from -1.5 to 2.5
- right_tensor: float32 [5, 5, 2, 2], replicated, may hold values from -1.5 to 2.5
Outputs:
- next_vector: bfloat16 [4, 2048, 2048], P(None, 'row', 'col')
- coefficients: float32 [2], replicated
All inputs are finite; a program needn't handle non-finite values.
Results may differ from a plain program's by a relative error of at most 0.023.
Values may be sent and summed in bfloat16 or wider, within the bound.
A program may use at most 64 MiB of HBM per device.

v0:
```python
import jax
import jax.numpy as jnp
from jax import lax
from jax.sharding import PartitionSpec as P

epsilon = 1e-06


def coupling(left_tensor, right_tensor):
    channels = left_tensor.shape[0]
    joined = jnp.einsum(
        "wuac,uvbd->vabwcd", left_tensor, right_tensor, precision=lax.Precision.HIGHEST
    )
    return joined.reshape(channels, 4, channels, 4)


def contract_left(portion, columns):
    return jnp.einsum("wax,txb->wtba", portion, columns, preferred_element_type=jnp.float32)


def mix_channels(coupling_table, cross):
    mixed_bond = jnp.einsum(
        "vswt,wtba->vsba", coupling_table, cross, precision=lax.Precision.HIGHEST
    )
    return mixed_bond.astype(jnp.bfloat16)


def contract_right(mixed_bond, portion):
    return jnp.einsum("vsba,vbc->sac", mixed_bond, portion, preferred_element_type=jnp.float32)


def apply_hamiltonian(vector, coupling_table, panels):
    columns = lax.all_gather(vector, "row", axis=1, tiled=True)
    cross = contract_left(panels[0], columns)
    mixed_bond = mix_channels(coupling_table, cross)
    partials = contract_right(mixed_bond, panels[1])
    return lax.psum_scatter(
        partials.astype(jnp.bfloat16), "col", scatter_dimension=2, tiled=True
    ).astype(jnp.float32)


def local_mean(former, latter, entries):
    return jnp.sum(former * latter) / entries


def body(start_vector, left_env, right_env, left_tensor, right_tensor):
    coupling_table = coupling(left_tensor, right_tensor)
    entries = float(
        start_vector.shape[0]
        * start_vector.shape[1]
        * start_vector.shape[2]
        * lax.axis_size("row")
        * lax.axis_size("col")
    )
    panels = (
        lax.all_gather(left_env, "col", axis=2, tiled=True),
        lax.all_gather(right_env, "row", axis=2, tiled=True),
    )
    base_vector = start_vector.astype(jnp.float32)
    image = apply_hamiltonian(start_vector, coupling_table, panels)
    base_square, correlation, image_square = lax.psum(
        (
            local_mean(base_vector, base_vector, entries),
            local_mean(base_vector, image, entries),
            local_mean(image, image, entries),
        ),
        ("row", "col"),
    )
    alpha = correlation / (base_square + epsilon)
    residual = image - alpha * base_vector
    rho = jnp.sqrt(image_square - 2.0 * alpha * correlation + alpha * alpha * base_square + epsilon)
    next_vector = (residual / rho).astype(jnp.bfloat16)
    coefficients = jnp.stack([alpha, rho])
    return (next_vector, coefficients)


def solution(mesh):
    return jax.shard_map(
        body,
        mesh=mesh,
        in_specs=(P(None, "row", "col"), P(None, "row", "col"), P(None, "col", "row"), P(), P()),
        out_specs=(P(None, "row", "col"), P()),
        check_vma=False,
    )
```

profile of v0, /device:TPU:24, one launch (start us, length us, event | category | flops | bytes accessed | tf_op | source)
XLA Modules:
  0.0 407.6 jit_solution(12811330662160053242)
XLA Ops:
  7.2 0.0 copy-start
  7.2 0.0 all-gather.4.cloned.1.call-start
  7.2 2.3 copy.15
  9.5 0.0 all-gather.4.cloned.1.call-update
  9.5 0.0 all-gather.6.cloned.1.call-start
  9.6 0.7 all-gather.6.cloned.1.call-update
  10.3 0.0 all-gather.8.cloned.1.call-start
  10.3 0.7 all-gather.8.cloned.1.call-update
  11.0 0.0 reduce-scatter.2.cloned.1.call-start
  11.1 0.0 copy-done
  11.1 0.0 copy-done.2
  11.1 0.4 convolution_bitcast_fusion
  11.6 52.3 %all-gather.4.cloned.1.call-done = bf16[4,2048,256]{1,2,0:T(8,128)(2,1)} async-done(((bf16[4,512,256]{1,2,0:T(8,128)(2,1)}), bf16[4,2048,256]{1,2,0:T(8,128)(2,1)}) %all-gather.4.cloned.1.call-update) | async-done | bytes 4194320 | tf_op jit(solution)/shard_map/all_gather | solution.py:33
  63.8 99.5 %all-gather.6.cloned.1.call-done = bf16[5,512,2048]{2,1,0:T(8,128)(2,1)} async-done(((bf16[5,512,256]{2,1,0:T(8,128)(2,1)}), bf16[5,512,2048]{2,1,0:T(8,128)(2,1)}) %all-gather.6.cloned.1.call-update) | async-done | bytes 10485776 | tf_op jit(solution)/shard_map/all_gather | solution.py:56
  163.3 15.1 %fusion.10 = f32[5,4,256,512]{3,2,0,1:T(8,128)S(1)} fusion(bf16[5,512,2048]{2,1,0:T(8,128)(2,1)} %all-gather.6.cloned.1.call-done, bf16[4,2048,256]{1,2,0:T(8,128)(2,1)} %all-gather.4.cloned.1.call-done), kind=kOutput, calls=%fused_computation.10 | convolution fusion | flops 10737418240 | bytes 25165824 | tf_op jit(solution)/shard_map/wax,txb->wtba/dot_general | solution.py:18
  178.4 66.0 %bitcast_convert_fusion.1 = bf16[5,4,256,512]{3,0,2,1:T(8,128)(2,1)} fusion(f32[5,4,256,512]{3,2,0,1:T(8,128)S(1)} %fusion.10, f32[5,4,5,4,1]{2,3,1,0,4:T(4,128)S(1)} %bitcast.38), kind=kOutput, calls=%fused_computation.1 | convolution fusion | flops 631767040 | bytes 15730240 | tf_op jit(solution)/shard_map/vswt,wtba->vsba/dot_general | solution.py:22
  244.4 19.3 %bitcast_convert_fusion = bf16[4,512,2048]{2,1,0:T(8,128)(2,1)} fusion(bf16[5,256,2048]{2,1,0:T(8,128)(2,1)} %all-gather.8.cloned.1.call-done, bf16[5,4,256,512]{3,0,2,1:T(8,128)(2,1)} %bitcast_convert_fusion.1), kind=kOutput, calls=%fused_computation | convolution fusion | flops 10741612544 | bytes 18874368 | tf_op jit(solution)/shard_map/vsba,vbc->sac/dot_general | solution.py:29
  263.7 0.0 reduce-scatter.2.cloned.1.call-update
  263.7 87.4 %reduce-scatter.2.cloned.1.call-done = bf16[4,512,256]{2,1,0:T(8,128)(2,1)} async-done(((bf16[4,512,2048]{2,1,0:T(8,128)(2,1)}), bf16[4,512,256]{2,1,0:T(8,128)(2,1)}) %reduce-scatter.2.cloned.1.call-update) | async-done | bytes 1048592 | tf_op jit(solution)/shard_map/reduce_scatter | solution.py:37
  351.1 0.0 copy-done.1
  351.1 2.5 fusion.19
  355.5 39.2 %all-reduce = (f32[]{:T(128)}, f32[]{:T(128)}, f32[]{:T(128)}) all-reduce(f32[]{:T(128)S(6)} %div.21, f32[]{:T(128)S(6)} %div.18, f32[]{:T(128)S(6)} %div.19), channel_id=1, replica_groups=mesh['row'=4,'col'=8] {'row','col'}, use_global_device_ids=true, to_apply=%region_6.0 | all-reduce | flops 3 | bytes 24 | tf_op jit(solution)/shard_map/psum | solution.py:61
  397.9 0.6 pad_maximum_fusion
  398.5 2.6 fusion.16
  (4 shorter events, 0.0 us)
Async XLA Ops:
  7.2 3.9 copy-start
  7.2 3.9 copy-start.2
  7.2 56.7 %all-gather.4.cloned.1.call-start = ((), (), s32[]{:S(2)}) async-start(), calls=%async_computation.1 | async-start | bytes 5242880 | tf_op jit(solution)/shard_map/all_gather | solution.py:33
  9.5 153.8 %all-gather.6.cloned.1.call-start = ((), (), s32[]{:S(2)}) async-start(), calls=%async_computation.2 | async-start | bytes 11796480 | tf_op jit(solution)/shard_map/all_gather | solution.py:56
  10.3 234.1 %all-gather.8.cloned.1.call-start = ((), (), s32[]{:S(2)}) async-start(), calls=%async_computation.3 | async-start | bytes 6553600 | tf_op jit(solution)/shard_map/all_gather | solution.py:57
  11.0 340.0 %reduce-scatter.2.cloned.1.call-start = ((), (), s32[]{:S(2)}) async-start(), calls=%async_computation.4 | async-start | bytes 9437184 | tf_op jit(solution)/shard_map/reduce_scatter | solution.py:37
  263.7 87.4 %copy-start.1 = (bf16[4,512,256]{2,1,0:T(8,128)(2,1)S(1)}, bf16[4,512,256]{2,1,0:T(8,128)(2,1)}, u32[]{:S(2)}) copy-start(bf16[4,512,256]{2,1,0:T(8,128)(2,1)} %param.5) | copy-start | bytes 3145732
Sparse Core Ops, SparseCore 0:
  10.4 53.4 all-gather.3
  65.4 97.8 all-gather.5
  165.2 61.2 all-gather.7
  263.8 87.1 reduce-scatter.1
where the time goes:
time: 411 us; the launch traced here: 408 us
  waiting for transfers between devices  241 us (59%)
  matrix products  101 us (25%)
  blocking collectives  39.2 us (10%)
  between operations  19 us (5%)
  other arithmetic  5.64 us (1%)
    all_gather x1, waiting for transfers between devices, body(): lax.all_gather(left_env, 'col', axis=2, tiled=True)  99.5 us
    reduce_scatter x1, waiting for transfers between devices, apply_hamiltonian(): lax.psum_scatter(partials.astype(jnp.bfloat16), 'col', scatter_dimension=...  87.4 us
    dot_general x1, matrix products, mix_channels(): jnp.einsum('vswt,wtba->vsba', coupling_table, cross, precision=lax.Precis...  66 us
    all_gather x1, waiting for transfers between devices, apply_hamiltonian(): columns = lax.all_gather(vector, 'row', axis=1, tiled=True)  52.3 us
    psum x1, blocking collectives, body(): lax.psum((local_mean(base_vector, base_vector, entries), local_mean(base_...  39.2 us
    dot_general x1, matrix products, contract_right(): jnp.einsum('vsba,vbc->sac', mixed_bond, portion, preferred_element_type=j...  19.3 us
    dot_general x1, matrix products, contract_left(): jnp.einsum('wax,txb->wtba', portion, columns, preferred_element_type=jnp....  15.1 us
  transfers between devices with their start and end apart: 4, of which 3 were waited for; matrix products, arithmetic and copies ran while one was open for 20% of the time, Pallas kernels for 0%

commit v1 on v0

--- a/solution.py
+++ b/solution.py
@@ -1,9 +1,16 @@
+import functools
+
 import jax
 import jax.numpy as jnp
 from jax import lax
+from jax.experimental import pallas as pl
+from jax.experimental.pallas import tpu as pltpu
 from jax.sharding import PartitionSpec as P
 
 epsilon = 1e-06
+PIECES = 4
+LAG = 2
+MESH = pl.DeviceIdType.MESH
 
 
 def coupling(left_tensor, right_tensor):
@@ -29,35 +36,494 @@
     return jnp.einsum("vsba,vbc->sac", mixed_bond, portion, preferred_element_type=jnp.float32)
 
 
-def apply_hamiltonian(vector, coupling_table, panels):
-    columns = lax.all_gather(vector, "row", axis=1, tiled=True)
-    cross = contract_left(panels[0], columns)
+def plain_image(start_vector, left_env, right_env, coupling_table):
+    left_panel = lax.all_gather(left_env, "col", axis=2, tiled=True)
+    right_panel = lax.all_gather(right_env, "row", axis=2, tiled=True)
+    columns = lax.all_gather(start_vector, "row", axis=1, tiled=True)
+    cross = contract_left(left_panel, columns)
     mixed_bond = mix_channels(coupling_table, cross)
-    partials = contract_right(mixed_bond, panels[1])
+    partials = contract_right(mixed_bond, right_panel)
     return lax.psum_scatter(
         partials.astype(jnp.bfloat16), "col", scatter_dimension=2, tiled=True
     ).astype(jnp.float32)
 
 
+def image_kernel(
+    layers, entries, table_ref, x_ref, l_ref, r_ref, next_ref, coef_ref,
+    xg, lg, rg, cross, mixed, pair_out, pair_in, chain_out, chain_in, total, image, stat_out, stat_in,
+    local_sem, l_send, l_recv, lp_send, lp_recv,
+    g_send, g_recv, d_send, d_recv, p_send, p_recv, c_send, c_recv, s_send, s_recv,
+):
+    states, rows, width = x_ref.shape
+    channels = l_ref.shape[0]
+    piece = rows // PIECES
+    row = lax.axis_index("row")
+    col = lax.axis_index("col")
+    layer = col // 2
+    core = col % 2
+    partner = (row, layer * 2 + (1 - core))
+    above = (row, (layer + 1) * 2 + core)
+    below = (row, (layer - 1) * 2 + core)
+    ways = (above, below)
+    sides = ((row // 2 * 2 + (1 - row % 2), col), (((row // 2) + 1) % 2 * 2 + row % 2, col))
+    side_rows = (sides[0][0], sides[1][0])
+    corner = ((row // 2) + 1) % 2 * 2 + (1 - row % 2)
+    has = (layer < layers - 1, layer > 0)
+    crossed = (row, ((layer + layers // 2) % layers) * 2 + core)
+    beside = (row, (layer // 2 * 2 + (1 - layer % 2)) * 2 + core)
+    rounds = (partner, beside, crossed) + sides
+
+    def remote(src, dst, send, recv, device):
+        return pltpu.make_async_remote_copy(
+            src_ref=src, dst_ref=dst, send_sem=send, recv_sem=recv,
+            device_id=device, device_id_type=MESH,
+        )
+
+    barrier = pltpu.get_barrier_semaphore()
+    for device in (partner, crossed) + sides:
+        pl.semaphore_signal(barrier, inc=1, device_id=device, device_id_type=MESH)
+    for w in range(2):
+        @pl.when(has[w])
+        def _():
+            pl.semaphore_signal(barrier, inc=1, device_id=ways[w], device_id_type=MESH)
+    pl.semaphore_wait(barrier, 4 + jnp.minimum(layer, 1) + jnp.minimum(layers - 1 - layer, 1))
+
+    def column(index, size):
+        return pl.ds(pl.multiple_of(index * size, size), size)
+
+    half = states // 2
+
+    def own_part(which, part):
+        if which == 0:
+            return x_ref.at[pl.ds(part * half, half)]
+        return r_ref.at[:, pl.ds(part * (width // 2), width // 2), :]
+
+    def held_part(which, source, part):
+        if which == 0:
+            return xg.at[pl.ds(part * half, half), column(source, rows), :]
+        return rg.at[source, :, pl.ds(part * (width // 2), width // 2), :]
+
+    def side_copy(which, side, part):
+        return remote(
+            own_part(which, part), held_part(which, row, part),
+            g_send.at[which, side, part], g_recv.at[which, side, part], sides[side],
+        )
+
+    def side_arrival(which, side, part):
+        return remote(
+            own_part(which, part), held_part(which, side_rows[side], part),
+            g_send.at[which, side, part], g_recv.at[which, side, part], sides[side],
+        )
+
+    def relay_copy(which, side):
+        part = held_part(which, side_rows[1 - side], side)
+        return remote(part, part, d_send.at[which, side], d_recv.at[which, side], sides[side])
+
+    def relay_arrival(which, side):
+        part = held_part(which, corner, side)
+        return remote(part, part, d_send.at[which, side], d_recv.at[which, side], sides[side])
+
+    def start_sides(which):
+        for side in range(2):
+            side_copy(which, side, 1 - side).start()
+        for side in range(2):
+            side_copy(which, side, side).start()
+
+    def start_relays(which):
+        for side in range(2):
+            side_arrival(which, 1 - side, side).wait_recv()
+            relay_copy(which, side).start()
+
+    def finish_sides(which):
+        for side in range(2):
+            side_arrival(which, side, side).wait_recv()
+
+    def finish_corner(which):
+        for side in range(2):
+            relay_arrival(which, side).wait_recv()
+
+    def own_left(k):
+        return l_ref.at[:, column(k, piece), :]
+
+    def held_left(k, owner):
+        return lg.at[k, :, :, column(owner, width)]
+
+    def left_copy(w, k, distance):
+        owner = (layer - distance if w == 0 else layer + distance) * 2 + core
+        source = own_left(k) if distance == 0 else held_left(k, owner)
+        return remote(
+            source, held_left(k, owner),
+            l_send.at[w, distance, k], l_recv.at[w, distance, k], ways[w],
+        )
+
+    def left_arrival(w, k, distance):
+        owner = (layer - distance if w == 0 else layer + distance) * 2 + core
+        part = held_left(k, owner)
+        return remote(
+            part, part, l_send.at[w, distance - 1, k], l_recv.at[w, distance - 1, k], ways[w]
+        )
+
+    def pair_left(k, owner_layer, own):
+        owner = owner_layer * 2 + core
+        source = own_left(k) if own else held_left(k, owner)
+        return remote(
+            source, held_left(k, owner),
+            lp_send.at[owner_layer, k], lp_recv.at[owner_layer, k], partner,
+        )
+
+    def pair_arrival(k, owner_layer):
+        part = held_left(k, owner_layer * 2 + (1 - core))
+        return remote(part, part, lp_send.at[owner_layer, k], lp_recv.at[owner_layer, k], partner)
+
+    def start_left(k):
+        for w in range(2):
+            @pl.when(has[w])
+            def _():
+                left_copy(w, k, 0).start()
+        pair_left(k, layer, True).start()
+
+    def reach(w, distance):
+        return layer >= distance if w == 0 else layer + distance < layers
+
+    def relay_left(k):
+        for distance in range(1, layers):
+            for w in range(2):
+                @pl.when(reach(w, distance))
+                def _():
+                    left_arrival(w, k, distance).wait_recv()
+                    if distance < layers - 1:
+                        @pl.when(has[w])
+                        def _():
+                            left_copy(w, k, distance).start()
+                    pair_left(k, layer - distance if w == 0 else layer + distance, False).start()
+
+    def own_copies():
+        return (
+            pltpu.make_async_copy(x_ref, xg.at[:, column(row, rows), :], local_sem.at[0]),
+            pltpu.make_async_copy(r_ref, rg.at[row], local_sem.at[1]),
+        )
+
+    def own_left_copy(k):
+        return pltpu.make_async_copy(own_left(k), held_left(k, col), local_sem.at[2 + k])
+
+    def multiply_left(k):
+        own_left_copy(k).wait()
+        for owner_layer in range(layers):
+            pair_arrival(k, owner_layer).wait_recv()
+
+        def state_step(t, carry):
+            left = lg[k].reshape(channels * piece, lg.shape[3])
+            product = jnp.dot(left, xg[t], preferred_element_type=jnp.float32)
+            cross[t] = product.reshape(channels, piece, width)
+            return carry
+
+        lax.fori_loop(0, states, state_step, 0)
+        lanes = width // 128
+
+        def mix_step(index, carry):
+            at = pl.ds(pl.multiple_of(index // lanes * 16, 16), 16)
+            lane = index % lanes * 128
+            taken = [
+                cross[t, w, at, pl.ds(pl.multiple_of(lane, 128), 128)]
+                for w in range(channels) for t in range(states)
+            ]
+            for v in range(channels):
+                for s in range(states):
+                    base = (v * states + s) * channels * states
+                    value = table_ref[base] * taken[0]
+                    for n in range(1, channels * states):
+                        value = value + table_ref[base + n] * taken[n]
+                    spot = pl.ds(pl.multiple_of(v * width + lane, 128), 128)
+                    mixed[k, s, at, spot] = value.astype(jnp.bfloat16)
+            return carry
+
+        lax.fori_loop(0, piece // 16 * lanes, mix_step, 0)
+
+    def pair_term(unit):
+        return remote(
+            pair_out.at[unit], pair_in.at[unit], p_send.at[unit], p_recv.at[unit], partner
+        )
+
+    def chain_term(w, unit):
+        return remote(
+            chain_out.at[unit], chain_in.at[w, unit], c_send.at[unit], c_recv.at[w, unit], ways[w]
+        )
+
+    def product_right(k, target, side):
+        left = mixed[k].reshape(states * piece, channels * width)
+        right = rg[target, :, :, column(side, width)].reshape(channels * width, width)
+        return jnp.dot(left, right, preferred_element_type=jnp.float32).reshape(
+            states, piece, width
+        )
+
+    def target_of(unit):
+        order = unit // PIECES
+        return (row // 2 + order // 2) % 2 * 2 + (row + order) % 2
+
+    slots = total.shape[0]
+
+    def send_on(unit, target):
+        for w in range(2):
+            @pl.when(layer < target if w == 0 else layer > target)
+            def _():
+                chain_out[unit] = total[unit % slots].astype(jnp.bfloat16)
+                chain_term(w, unit).start()
+
+    def make_unit(unit):
+        k = unit % PIECES
+        target = target_of(unit)
+        pair_out[unit] = product_right(k, target, 1 - core).astype(jnp.bfloat16)
+        pair_term(unit).start()
+        total[unit % slots] = product_right(k, target, core)
+        pair_term(unit).wait_recv()
+        total[unit % slots] += pair_in[unit].astype(jnp.float32)
+
+    def join_unit(unit):
+        k = unit % PIECES
+        target = target_of(unit)
+        slot = unit % slots
+        for w in range(2):
+            ahead = layer <= target if w == 0 else layer >= target
+
+            @pl.when(has[1 - w] & ahead)
+            def _():
+                chain_term(w, unit).wait_recv()
+                total[slot] += chain_in[w, unit].astype(jnp.float32)
+        send_on(unit, target)
+
+        @pl.when(layer == target)
+        def _():
+            image[:, column(k, piece), :] = total[slot]
+
+    def join_step(step):
+        for hops in range(layers - 1, -1, -1):
+            unit = step - hops * LAG
+
+            @pl.when((unit >= 0) & (unit < layers * PIECES))
+            def _():
+                target = target_of(unit)
+                low = jnp.minimum(layer, layers - 1 - layer)
+                high = layers - 1 - low
+                up, down = layer, layers - 1 - layer
+                fits = (
+                    ((layer < target) & (up == hops))
+                    | ((layer > target) & (down == hops))
+                    | ((layer == target) & (high == hops))
+                )
+
+                @pl.when(fits)
+                def _():
+                    join_unit(unit)
+
+    for copy in own_copies():
+        copy.start()
+    for k in range(PIECES):
+        own_left_copy(k).start()
+    start_left(0)
+    start_sides(0)
+    start_left(1)
+    start_relays(0)
+    start_sides(1)
+    relay_left(0)
+    start_left(2)
+    finish_sides(0)
+    finish_corner(0)
+    for copy in own_copies():
+        copy.wait()
+
+    def piece_step(k, carry):
+        @pl.when(k < PIECES - 1)
+        def _():
+            relay_left(k + 1)
+
+        @pl.when(k < PIECES - 3)
+        def _():
+            start_left(k + 3)
+
+        multiply_left(k)
+        make_unit(k)
+        join_step(k)
+
+        @pl.when(k == 1)
+        def _():
+            start_relays(1)
+
+        return carry
+
+    lax.fori_loop(0, PIECES, piece_step, 0)
+    finish_sides(1)
+
+    def unit_step(unit, carry):
+        @pl.when(unit == 3 * PIECES)
+        def _():
+            finish_corner(1)
+
+        @pl.when(unit < layers * PIECES)
+        def _():
+            make_unit(unit)
+
+        join_step(unit)
+        return carry
+
+    lax.fori_loop(PIECES, layers * PIECES + (layers - 1) * LAG, unit_step, 0)
+
+    def sum_step(index, sums):
+        at = pl.ds(pl.multiple_of(index * 8, 8), 8)
+        base_square, correlation, image_square = sums
+        for t in range(states):
+            former = x_ref[t, at, :].astype(jnp.float32)
+            latter = image[t, at, :]
+            base_square = base_square + former * former
+            correlation = correlation + former * latter
+            image_square = image_square + latter * latter
+        return base_square, correlation, image_square
+
+    nothing = jnp.zeros((8, width), jnp.float32)
+    sums = lax.fori_loop(0, rows // 8, sum_step, (nothing, nothing, nothing))
+    for n in range(3):
+        stat_out[0, n] = jnp.sum(sums[n].reshape(8, width // 128, 128), axis=1) / entries
+    for number, device in enumerate(rounds):
+        swap = remote(
+            stat_out.at[number], stat_in.at[number], s_send.at[number], s_recv.at[number], device
+        )
+        swap.start()
+        swap.wait_recv()
+        stat_out[number + 1] = stat_out[number] + stat_in[number]
+    base_square, correlation, image_square = (
+        jnp.sum(stat_out[len(rounds), n], axis=(0, 1), keepdims=True) for n in range(3)
+    )
+    alpha = correlation / (base_square + epsilon)
+    square = image_square - 2.0 * alpha * correlation + alpha * alpha * base_square
+    rho = jnp.sqrt(square + epsilon)
+    coef_ref[0] = jnp.broadcast_to(alpha, (8, 128))
+    coef_ref[1] = jnp.broadcast_to(rho, (8, 128))
+
+    def scale_step(index, carry):
+        at = pl.ds(pl.multiple_of(index * 16, 16), 16)
+        for t in range(states):
+            residual = image[t, at, :] - alpha * x_ref[t, at, :].astype(jnp.float32)
+            next_ref[t, at, :] = (residual / rho).astype(jnp.bfloat16)
+        return carry
+
+    lax.fori_loop(0, rows // 16, scale_step, 0)
+    for number, device in enumerate(rounds):
+        remote(
+            stat_out.at[number], stat_in.at[number], s_send.at[number], s_recv.at[number], device
+        ).wait_send()
+
+    for which in range(2):
+        for side in range(2):
+            side_copy(which, side, 0).wait_send()
+            side_copy(which, side, 1).wait_send()
+            relay_copy(which, side).wait_send()
+
+    def left_end(k, carry):
+        pair_left(k, layer, True).wait_send()
+        for w in range(2):
+            @pl.when(has[w])
+            def _():
+                left_copy(w, k, 0).wait_send()
+        for distance in range(1, layers):
+            for w in range(2):
+                @pl.when(reach(w, distance))
+                def _():
+                    if distance < layers - 1:
+                        @pl.when(has[w])
+                        def _():
+                            left_copy(w, k, distance).wait_send()
+                    pair_left(k, layer - distance if w == 0 else layer + distance, False).wait_send()
+        return carry
+
+    lax.fori_loop(0, PIECES, left_end, 0)
+
+    def unit_end(unit, carry):
+        target = target_of(unit)
+        pair_term(unit).wait_send()
+        for w in range(2):
+            @pl.when(layer < target if w == 0 else layer > target)
+            def _():
+                chain_term(w, unit).wait_send()
+        return carry
+
+    lax.fori_loop(0, 4 * PIECES, unit_end, 0)
+
+
+def linked_step(start_vector, left_env, right_env, coupling_table, entries):
+    states, rows, width = start_vector.shape
+    channels = left_env.shape[0]
+    sources = lax.axis_size("row")
+    owners = lax.axis_size("col")
+    layers = owners // 2
+    piece = rows // PIECES
+    units = layers * PIECES
+    narrow = jnp.bfloat16
+    dma = pltpu.SemaphoreType.DMA
+    return pl.pallas_call(
+        functools.partial(image_kernel, layers, entries),
+        out_shape=(
+            jax.ShapeDtypeStruct((states, rows, width), narrow),
+            jax.ShapeDtypeStruct((2, 8, 128), jnp.float32),
+        ),
+        in_specs=[pl.BlockSpec(memory_space=pltpu.SMEM)]
+        + [pl.BlockSpec(memory_space=pltpu.VMEM)] * 3,
+        out_specs=(pl.BlockSpec(memory_space=pltpu.VMEM),) * 2,
+        scratch_shapes=[
+            pltpu.VMEM((states, sources * rows, width), narrow),
+            pltpu.VMEM((PIECES, channels, piece, owners * width), narrow),
+            pltpu.VMEM((sources, channels, width, right_env.shape[2]), narrow),
+            pltpu.VMEM((states, channels, piece, width), jnp.float32),
+            pltpu.VMEM((PIECES, states, piece, channels * width), narrow),
+            pltpu.VMEM((units, states, piece, width), narrow),
+            pltpu.VMEM((units, states, piece, width), narrow),
+            pltpu.VMEM((units, states, piece, width), narrow),
+            pltpu.VMEM((2, units, states, piece, width), narrow),
+            pltpu.VMEM((8, states, piece, width), jnp.float32),
+            pltpu.VMEM((states, rows, width), jnp.float32),
+            pltpu.VMEM((6, 3, 8, 128), jnp.float32),
+            pltpu.VMEM((5, 3, 8, 128), jnp.float32),
+            dma((2 + PIECES,)),
+            dma((2, layers, PIECES)),
+            dma((2, layers, PIECES)),
+            dma((layers, PIECES)),
+            dma((layers, PIECES)),
+            dma((2, 2, 2)),
+            dma((2, 2, 2)),
+            dma((2, 2)),
+            dma((2, 2)),
+            dma((units,)),
+            dma((units,)),
+            dma((units,)),
+            dma((2, units)),
+            dma((5,)),
+            dma((5,)),
+        ],
+        compiler_params=pltpu.CompilerParams(
+            collective_id=0, has_side_effects=True, vmem_limit_bytes=65000 * 1024
+        ),
+    )(coupling_table.reshape(-1), start_vector, left_env, right_env)
+
+
 def local_mean(former, latter, entries):
     return jnp.sum(former * latter) / entries
 
 
 def body(start_vector, left_env, right_env, left_tensor, right_tensor):
     coupling_table = coupling(left_tensor, right_tensor)
-    entries = float(
-        start_vector.shape[0]
-        * start_vector.shape[1]
-        * start_vector.shape[2]
-        * lax.axis_size("row")
-        * lax.axis_size("col")
+    states, rows, width = start_vector.shape
+    sources = lax.axis_size("row")
+    owners = lax.axis_size("col")
+    entries = float(states * rows * width * sources * owners)
+    planned = (
+        sources == 4 and owners == 2 * sources and width % 128 == 0
+        and rows % (PIECES * 16) == 0 and states % 2 == 0
     )
-    panels = (
-        lax.all_gather(left_env, "col", axis=2, tiled=True),
-        lax.all_gather(right_env, "row", axis=2, tiled=True),
-    )
+    if planned:
+        next_vector, numbers = linked_step(
+            start_vector, left_env, right_env, coupling_table, entries
+        )
+        return (next_vector, numbers[:, 0, 0])
     base_vector = start_vector.astype(jnp.float32)
-    image = apply_hamiltonian(start_vector, coupling_table, panels)
+    image = plain_image(start_vector, left_env, right_env, coupling_table)
     base_square, correlation, image_square = lax.psum(
         (
             local_mean(base_vector, base_vector, entries),

time: 411 us -> 234 us (0.57)
  waiting for transfers between devices: 241 us -> 0 us
  Pallas kernels: 0 us -> 227 us
  matrix products: 101 us -> 1.11 us
  blocking collectives: 39.2 us -> 0 us
  between operations: 19 us -> 0.66 us
  other arithmetic: 5.64 us -> 0 us
    pallas_call x0 -> x1, Pallas kernels: none -> 227 us  [linked_step(): pl.pallas_call(functools.partial(image_kernel, layers, entries), out_shap...]
    all_gather x3 -> x0, waiting for transfers between devices: 152 us -> none  [the longest x1 99.5 us: body(): lax.all_gather(left_env, 'col', axis=2, tiled=True)]
    dot_general x3 -> x0, matrix products: 100 us -> none  [the longest x1 66 us: mix_channels(): jnp.einsum('vswt,wtba->vsba', coupling_table, cross, precision=lax.Precis...]
    reduce_scatter x1 -> x0, waiting for transfers between devices: 87.4 us -> none  [apply_hamiltonian(): lax.psum_scatter(partials.astype(jnp.bfloat16), 'col', scatter_dimension=...]
    psum x1 -> x0, blocking collectives: 39.2 us -> none  [body(): lax.psum((local_mean(base_vector, base_vector, entries), local_mean(base_...]
  transfers between devices with their start and end apart: 4 -> 0, of which waited for: 3 -> 0; matrix products, arithmetic and copies ran while one was open for 20% -> 0% of each run, Pallas kernels for 0% -> 0%
where the time goes in v1:
time: 234 us
  Pallas kernels  227 us (97%)
  local copies, waits for them, and re-layouts  5.37 us (2%)
    pallas_call x1, Pallas kernels, linked_step(): pl.pallas_call(functools.partial(image_kernel, layers, entries), out_shap...  227 us

profile of v1, /device:TPU:24, one launch (start us, length us, event | category | flops | bytes accessed | tf_op | source)
XLA Modules:
  0.0 233.8 jit_solution(11224490497374371420)
XLA Ops:
  0.6 0.0 copy-start
  0.6 0.7 copy-done
  1.3 1.1 convolution_bitcast_fusion
  2.5 0.4 copy.11
  2.8 0.7 reshape_reshape.3.table_ref
  3.6 226.7 %shard_map.68 = (bf16[4,512,256]{2,1,0:T(8,128)(2,1)}, f32[2,8,128]{2,1,0:T(8,128)}) custom-call(f32[400]{0:T(512)} %reshape_reshape.3.table_ref, bf16[4,512,256]{2,1,0:T(8,128)(2,1)} %x_ref.1, bf16[5,512,256]{2,1,0:T(8,128)(2,1)} %l_ref.1, bf16[5,256,512]{2,1,0:T(8,128)(2,1)} %r_ref.1), custom_call_target="tpu_custom_call" | custom-call | tf_op jit(solution)/shard_map/pallas_call | solution.py:461
  230.3 1.3 slice_reduce_fusion
  231.6 2.3 copy.23
Async XLA Ops:
  0.6 0.7 copy-start

commit v2 on v1

--- a/solution.py
+++ b/solution.py
@@ -185,17 +185,21 @@
     def reach(w, distance):
         return layer >= distance if w == 0 else layer + distance < layers
 
-    def relay_left(k):
-        for distance in range(1, layers):
-            for w in range(2):
-                @pl.when(reach(w, distance))
-                def _():
-                    left_arrival(w, k, distance).wait_recv()
-                    if distance < layers - 1:
-                        @pl.when(has[w])
-                        def _():
-                            left_copy(w, k, distance).start()
-                    pair_left(k, layer - distance if w == 0 else layer + distance, False).start()
+    def relay_hop(k, distance):
+        for w in range(2):
+            @pl.when(reach(w, distance))
+            def _():
+                left_arrival(w, k, distance).wait_recv()
+                if distance < layers - 1:
+                    @pl.when(has[w])
+                    def _():
+                        left_copy(w, k, distance).start()
+                pair_left(k, layer - distance if w == 0 else layer + distance, False).start()
+
+    def relay_later(k, distance):
+        @pl.when(k < PIECES)
+        def _():
+            relay_hop(k, distance)
 
     def own_copies():
         return (
@@ -218,6 +222,8 @@
             return carry
 
         lax.fori_loop(0, states, state_step, 0)
+        for distance in range(2, layers - 1):
+            relay_later(k + 1, distance)
         lanes = width // 128
 
         def mix_step(index, carry):
@@ -324,7 +330,8 @@
     start_left(1)
     start_relays(0)
     start_sides(1)
-    relay_left(0)
+    for distance in range(1, layers):
+        relay_hop(0, distance)
     start_left(2)
     finish_sides(0)
     finish_corner(0)
@@ -332,15 +339,14 @@
         copy.wait()
 
     def piece_step(k, carry):
-        @pl.when(k < PIECES - 1)
-        def _():
-            relay_left(k + 1)
+        relay_later(k + 1, 1)
 
         @pl.when(k < PIECES - 3)
         def _():
             start_left(k + 3)
 
         multiply_left(k)
+        relay_later(k + 1, layers - 1)
         make_unit(k)
         join_step(k)
 

time: 234 us -> 220 us (0.940)
  Pallas kernels: 227 us -> 213 us
    pallas_call x1, Pallas kernels: 227 us -> 213 us  [linked_step(): pl.pallas_call(functools.partial(image_kernel, layers, entries), out_shap...]
where the time goes in v2:
time: 220 us
  Pallas kernels  213 us (97%)
  local copies, waits for them, and re-layouts  5.37 us (2%)
    pallas_call x1, Pallas kernels, linked_step(): pl.pallas_call(functools.partial(image_kernel, layers, entries), out_shap...  213 us

profile of v2, /device:TPU:24, one launch (start us, length us, event | category | flops | bytes accessed | tf_op | source)
XLA Modules:
  0.0 219.7 jit_solution(3430324667261035818)
XLA Ops:
  0.6 0.0 copy-start
  0.6 0.7 copy-done
  1.3 1.1 convolution_bitcast_fusion
  2.5 0.4 copy.11
  2.8 0.7 reshape_reshape.3.table_ref
  3.6 212.6 %shard_map.68 = (bf16[4,512,256]{2,1,0:T(8,128)(2,1)}, f32[2,8,128]{2,1,0:T(8,128)}) custom-call(f32[400]{0:T(512)} %reshape_reshape.3.table_ref, bf16[4,512,256]{2,1,0:T(8,128)(2,1)} %x_ref.1, bf16[5,512,256]{2,1,0:T(8,128)(2,1)} %l_ref.1, bf16[5,256,512]{2,1,0:T(8,128)(2,1)} %r_ref.1), custom_call_target="tpu_custom_call" | custom-call | tf_op jit(solution)/shard_map/pallas_call | solution.py:467
  216.2 1.3 slice_reduce_fusion
  217.5 2.3 %copy.23 = bf16[4,512,256]{2,1,0:T(8,128)(2,1)} copy(bf16[4,512,256]{2,1,0:T(8,128)(2,1)} %get-tuple-element.8) | data formatting | bytes 2097152
Async XLA Ops:
  0.6 0.7 copy-start
